TPU v7x, 32 devices: a whole 2x2x4 slice. The times are simulated.
32 devices in a mesh: dp: 8 (over z, x), mp: 4 (over y, core).
Axes of the slice: x: 2, y: 2, z: 4, core: 2. Of those that a mesh axis runs over, the one named last changes fastest.
Arguments:
- tokens: bfloat16 [2048, 2048], P('dp'), may hold values from -6 to 6
- targets: bfloat16 [2048, 2048], P('dp'), may hold values from -6 to 6
- loss_weights: float32 [2048], P('dp'), may hold values from 0.4 to 14, as said below
- segments: int32 [8, 256], P('dp'), may hold values from 0 to 3, never falling along the last dimension, each value on 1 to 128 neighbouring positions
- probe_model: int32 [8, 2048], P('dp'), may hold values from 0 to 1
- probe_heads: int32 [8, 2, 2048], P('dp', None, 'mp'), may hold values from 0 to 1
- norm_gain: float32 [2048], replicated, may hold values from 0.5 to 1.5
- w_query: bfloat16 [2048, 2048], P(None, 'mp'), may hold values from -0.125 to 0.125
- w_key: bfloat16 [2048, 2048], P(None, 'mp'), may hold values from -0.125 to 0.125
- w_value: bfloat16 [2048, 2048], P(None, 'mp'), may hold values from -0.125 to 0.125
- w_out: bfloat16 [2048, 2048], P('mp'), may hold values from -0.125 to 0.125
Outputs:
- diag_query: float32 [2048, 2048], P('dp', 'mp')
- diag_key: float32 [2048, 2048], P('dp', 'mp')
- mean_diag: float32 [2], replicated
Inputs may be any that keep to these rules, and one draw needn't show every extreme that they name: `segments`: the documents of a sequence are runs of 1 to 128 tokens, numbered upwards from 0. `loss_weights`: positive weights.
All inputs are finite; a program needn't handle non-finite values.
Results may differ from a plain program's by a relative error of at most 0.0099.
Values may be sent and summed in bfloat16 or wider, within the bound.
A program may use at most 128 MiB of HBM per device.

v0:
```python
import functools

import jax
import jax.numpy as jnp
from jax import lax
from jax.experimental import pallas as pl
from jax.experimental.pallas import tpu as pltpu
from jax.sharding import PartitionSpec as P

HEAD_DIM = 128
PRIME = 32749
CHUNKS = 2
EXACT = lax.Precision.HIGHEST
F32 = jnp.float32
BF16 = jnp.bfloat16
MESH = pl.DeviceIdType.MESH

NN = (((1,), (0,)), ((), ()))
NT = (((1,), (1,)), ((), ()))
TN = (((0,), (0,)), ((), ()))


def dot(left, right, dims=NN, precision=None):
    return lax.dot_general(left, right, dims, precision=precision, preferred_element_type=F32)


def low(left, right, dims=NN):
    return dot(left.astype(BF16), right.astype(BF16), dims)


def residue(whole):
    value = whole.astype(F32)
    left = value - jnp.floor(value * (1.0 / PRIME)) * PRIME
    left = jnp.where(left < 0, left + PRIME, left)
    left = jnp.where(left >= PRIME, left - PRIME, left)
    return left.astype(jnp.int32)


def pattern_block(row_part, col_part):
    mixed = row_part + col_part
    mixed = jnp.where(mixed >= PRIME, mixed - PRIME, mixed)
    square = mixed * mixed
    times = (square.astype(F32) * (1.0 / PRIME)).astype(jnp.int32)
    left = square - times * PRIME
    left = jnp.where(left < 0, left + PRIME, left)
    left = jnp.where(left >= PRIME, left - PRIME, left)
    odd = jnp.bitwise_and(jnp.right_shift(left * 52429, 18), 1)
    return jnp.where(odd == 1, -1.0, 1.0).astype(BF16)


def kernel(
    groups,
    parts,
    entries,
    tokens,
    targets,
    row_weights,
    seg_col,
    seg_row,
    model_sign,
    head_sign,
    gain,
    cosine,
    sine,
    wq_hbm,
    wk_hbm,
    wv_hbm,
    wo_hbm,
    diag_query,
    diag_key,
    mean_out,
    wq,
    wk,
    wv,
    wo,
    normed,
    signed,
    turned,
    turned_all,
    pattern,
    query,
    keys,
    values,
    product,
    soft,
    d_soft,
    attended,
    out_send,
    own_part,
    pair_recv,
    chip_send,
    chip_recv,
    residual,
    hk_sum,
    gathered,
    stat_send,
    stat_recv,
    stat_all,
    w_sem,
    turn_send,
    turn_recv,
    pair_ssem,
    pair_rsem,
    chip_ssem,
    chip_rsem,
    res_ssem,
    res_rsem,
    line_ssem,
    line_rsem,
    x_ssem,
    stat_ssem,
    stat_rsem,
    all_ssem,
    all_rsem,
):
    seq, width = tokens.shape
    feat = wq.shape[1]
    heads = feat // HEAD_DIM
    block = width // groups
    rows = seq // CHUNKS
    dp = lax.axis_index("dp")
    mp = lax.axis_index("mp")
    kind = lax.rem(mp, 2)
    other = 1 - kind
    pair = mp + 1 - 2 * kind
    chip = lax.rem(mp + 2, parts)
    inner = lax.rem(dp, 2)
    outer = dp // 2
    lines = groups // 2
    x_peer = dp + 1 - 2 * inner

    loads = []
    for n, (source, target) in enumerate(((wq_hbm, wq), (wk_hbm, wk), (wv_hbm, wv), (wo_hbm, wo))):
        load = pltpu.make_async_copy(source, target, w_sem.at[n])
        load.start()
        loads.append(load)

    barrier = pltpu.get_barrier_semaphore()
    for step in range(1, groups):
        pl.semaphore_signal(barrier, inc=1, device_id={"dp": lax.rem(dp + step, groups)}, device_id_type=MESH)
    pl.semaphore_signal(barrier, inc=1, device_id={"mp": pair}, device_id_type=MESH)
    pl.semaphore_signal(barrier, inc=1, device_id={"mp": chip}, device_id_type=MESH)

    token_float = tokens[...].astype(F32)
    inverse = lax.rsqrt(jnp.sum(token_float * token_float, axis=1, keepdims=True) / width + 1e-06)
    for start in range(0, width, 256):
        cols = slice(start, start + 256)
        part = (tokens[:, cols].astype(F32) * inverse * gain[:, cols]).astype(BF16)
        normed[:, cols] = part
        part_signed = part.astype(F32) * model_sign[:, cols]
        signed[:, cols] = part_signed.astype(BF16)
        turned[start : start + 256, :] = jnp.transpose(part_signed).astype(BF16)

    pl.semaphore_wait(barrier, groups + 1)

    turns = []
    for step in range(1, groups):
        peer = lax.rem(dp + step, groups)
        turn = pltpu.make_async_remote_copy(
            src_ref=turned.at[pl.ds(pl.multiple_of(peer * block, block), block), :],
            dst_ref=turned_all.at[dp],
            send_sem=turn_send.at[step],
            recv_sem=turn_recv.at[step],
            device_id={"dp": peer},
            device_id_type=MESH,
        )
        turn.start()
        turns.append(turn)

    first_col = mp * feat
    col_part = residue((first_col + lax.broadcasted_iota(jnp.int32, (1, feat), 1)) * 2713)
    total = jnp.zeros((seq, feat), F32)
    for start in range(0, width, 256):
        row_part = residue((start + lax.broadcasted_iota(jnp.int32, (256, 1), 0)) * 1103 + 7)
        signs = pattern_block(row_part, col_part)
        pattern[start : start + 256, :] = signs
        total = total + dot(signed[:, start : start + 256], signs)
    product[...] = total
    loads[0].wait()
    query[...] = dot(normed[...], wq[...])
    loads[1].wait()
    keys[...] = dot(normed[...], wk[...])
    loads[2].wait()
    values[...] = dot(normed[...], wv[...])

    cos = cosine[...]
    sin = sine[...]

    def rotate(array, cos_rows, sin_rows):
        return array * cos_rows + pltpu.roll(array, HEAD_DIM // 2, 1) * sin_rows

    def unrotate(array, cos_rows, sin_rows):
        return array * cos_rows - pltpu.roll(array, HEAD_DIM // 2, 1) * sin_rows

    scale = HEAD_DIM ** (-0.5)
    position_q = lax.broadcasted_iota(jnp.int32, (seq, seq), 0)
    position_k = lax.broadcasted_iota(jnp.int32, (seq, seq), 1)
    allowed = (position_q >= position_k) & (seg_col[...] == seg_row[...])
    for h in range(heads):
        cols = slice(h * HEAD_DIM, (h + 1) * HEAD_DIM)
        q = rotate(query[:, cols], cos, sin)
        k = rotate(keys[:, cols], cos, sin)
        probe = product[:, cols]
        dq = rotate(probe * head_sign[0:1, cols], cos, sin)
        dk = rotate(probe * head_sign[1:2, cols], cos, sin)
        scores = dot(q, k, NT, EXACT) * scale
        d_scores = dot(
            jnp.concatenate([dq, q], axis=1), jnp.concatenate([k, dk], axis=1), NT, EXACT
        ) * scale
        raised = jnp.where(allowed, jnp.exp(scores), 0.0)
        p = raised / jnp.sum(raised, axis=1, keepdims=True)
        d_p = p * (d_scores - jnp.sum(p * d_scores, axis=1, keepdims=True))
        soft[h] = p
        d_soft[h] = d_p
        v = values[:, cols]
        attended[0, :, cols] = low(p, v).astype(BF16)
        attended[1, :, cols] = low(d_p, v).astype(BF16)

    loads[3].wait()

    def pair_copy(c):
        return pltpu.make_async_remote_copy(
            src_ref=out_send.at[pl.ds(c * rows, rows), :],
            dst_ref=pair_recv.at[pl.ds(c * rows, rows), :],
            send_sem=pair_ssem.at[c],
            recv_sem=pair_rsem.at[c],
            device_id={"mp": pair},
            device_id_type=MESH,
        )

    def chip_copy(c):
        return pltpu.make_async_remote_copy(
            src_ref=chip_send.at[pl.ds(c * rows, rows), :],
            dst_ref=chip_recv.at[pl.ds(c * rows, rows), :],
            send_sem=chip_ssem.at[c],
            recv_sem=chip_rsem.at[c],
            device_id={"mp": chip},
            device_id_type=MESH,
        )

    def res_copy(c, which):
        return pltpu.make_async_remote_copy(
            src_ref=residual.at[which, pl.ds(c * rows, rows), :],
            dst_ref=residual.at[which, pl.ds(c * rows, rows), :],
            send_sem=res_ssem.at[c],
            recv_sem=res_rsem.at[c],
            device_id={"mp": pair},
            device_id_type=MESH,
        )

    order = list(range(CHUNKS))[::-1]
    for c in order:
        span = slice(c * rows, (c + 1) * rows)
        out_send[span, :] = dot(attended[other, span, :], wo[...]).astype(BF16)
        pair_copy(c).start()
        own_part[span, :] = dot(attended[kind, span, :], wo[...])
    for c in order:
        span = slice(c * rows, (c + 1) * rows)
        pair_copy(c).wait_recv()
        summed = own_part[span, :] + pair_recv[span, :].astype(F32)
        own_part[span, :] = summed
        chip_send[span, :] = summed.astype(BF16)
        chip_copy(c).start()

    def line_copy(c, slot, target, way):
        return pltpu.make_async_remote_copy(
            src_ref=gathered.at[c, slot],
            dst_ref=gathered.at[c, slot],
            send_sem=line_ssem.at[c, way, slot],
            recv_sem=line_rsem.at[c, slot],
            device_id={"dp": target},
            device_id_type=MESH,
        )

    def x_copy(c, slot):
        return pltpu.make_async_remote_copy(
            src_ref=gathered.at[c, slot],
            dst_ref=gathered.at[c, slot],
            send_sem=x_ssem.at[c, slot],
            recv_sem=line_rsem.at[c, slot],
            device_id={"dp": x_peer},
            device_id_type=MESH,
        )

    def send_own(c):
        @pl.when(outer + 1 < lines)
        def _():
            line_copy(c, dp, dp + 2, 0).start()

        @pl.when(outer >= 1)
        def _():
            line_copy(c, dp, dp - 2, 1).start()

        x_copy(c, dp).start()

    def relay(c, step):
        @pl.when(outer - step >= 0)
        def _():
            slot = dp - 2 * step
            line_copy(c, slot, dp, 0).wait_recv()

            @pl.when(outer + 1 < lines)
            def _():
                line_copy(c, slot, dp + 2, 0).start()

            x_copy(c, slot).start()

        @pl.when(outer + step < lines)
        def _():
            slot = dp + 2 * step
            line_copy(c, slot, dp, 1).wait_recv()

            @pl.when(outer >= 1)
            def _():
                line_copy(c, slot, dp - 2, 1).start()

            x_copy(c, slot).start()

    wanted = jnp.where(kind == 0, 1.0, 0.0)
    sum_q = jnp.zeros((1, HEAD_DIM), F32)
    sum_k = jnp.zeros((1, HEAD_DIM), F32)
    for c in order:
        span = slice(c * rows, (c + 1) * rows)
        reach = (c + 1) * rows
        chip_copy(c).wait_recv()
        whole = own_part[span, :] + chip_recv[span, :].astype(F32)
        shift = tokens[span, :].astype(F32) - targets[span, :].astype(F32)
        residual[kind, span, :] = ((whole + wanted * shift) * row_weights[span, :]).astype(BF16)
        res_copy(c, kind).start()
        back_own = dot(residual[kind, span, :], wo[...], NT)
        res_copy(c, other).wait_recv()
        back_other = dot(residual[other, span, :], wo[...], NT)
        back = jnp.where(kind == 0, back_own, back_other)
        back_tangent = jnp.where(kind == 0, back_other, back_own)
        cos_q = cos[span, :]
        sin_q = sin[span, :]
        cos_k = cos[:reach, :]
        sin_k = sin[:reach, :]
        for h in range(heads):
            cols = slice(h * HEAD_DIM, (h + 1) * HEAD_DIM)
            q = rotate(query[span, cols], cos_q, sin_q)
            k = rotate(keys[:reach, cols], cos_k, sin_k)
            dq = rotate(product[span, cols] * head_sign[0:1, cols], cos_q, sin_q)
            dk = rotate(product[:reach, cols] * head_sign[1:2, cols], cos_k, sin_k)
            v = values[:reach, cols]
            p = soft[h, span, :reach]
            d_p = d_soft[h, span, :reach]
            u = low(back[:, cols], v, NT)
            u_tangent = low(back_tangent[:, cols], v, NT)
            centered = u - jnp.sum(p * u, axis=1, keepdims=True)
            level = jnp.sum(d_p * u + p * u_tangent, axis=1, keepdims=True)
            mixed = (d_p * centered + p * (u_tangent - level)) * scale
            first = p * centered * scale
            both = jnp.concatenate([mixed, first], axis=1)
            hq = unrotate(low(both, jnp.concatenate([k, dk], axis=0)), cos_q, sin_q)
            stacked = jnp.concatenate([mixed, first], axis=0)
            hk = low(stacked, jnp.concatenate([q, dq], axis=0), TN)
            if c == CHUNKS - 1:
                hk_sum[:, cols] = hk
            else:
                hk_sum[:reach, cols] = hk_sum[:reach, cols] + hk
            hk = unrotate(hk_sum[span, cols], cos_q, sin_q)
            hq = (hq.astype(BF16).astype(F32) * head_sign[0:1, cols]).astype(BF16)
            hk = (hk.astype(BF16).astype(F32) * head_sign[1:2, cols]).astype(BF16)
            gathered[c, dp, :, cols] = hq
            gathered[c, dp, :, slice(feat + h * HEAD_DIM, feat + (h + 1) * HEAD_DIM)] = hk
            probe = product[span, cols]
            sum_q = sum_q + jnp.sum(hq.astype(F32) * probe, axis=0, keepdims=True)
            sum_k = sum_k + jnp.sum(hk.astype(F32) * probe, axis=0, keepdims=True)
        send_own(c)
        if c != order[-1]:
            relay(c, 1)

    lane = lax.broadcasted_iota(jnp.int32, (1, HEAD_DIM), 1)
    local = jnp.where(
        lane < HEAD_DIM // 2,
        jnp.sum(sum_q, axis=1, keepdims=True),
        jnp.sum(sum_k, axis=1, keepdims=True),
    )

    def stat_copy(n, peer):
        return pltpu.make_async_remote_copy(
            src_ref=stat_send.at[n],
            dst_ref=stat_recv.at[n],
            send_sem=stat_ssem.at[n],
            recv_sem=stat_rsem.at[n],
            device_id={"mp": peer},
            device_id_type=MESH,
        )

    stat_send[0] = local
    stat_copy(0, pair).start()
    for c in order[:-1]:
        for step in range(2, lines):
            relay(c, step)
    stat_copy(0, pair).wait_recv()
    stat_send[1] = stat_send[0] + stat_recv[0]
    stat_copy(1, chip).start()
    relay(order[-1], 1)
    stat_copy(1, chip).wait_recv()
    stat_all[dp] = stat_send[1] + stat_recv[1]

    def all_copy(step):
        return pltpu.make_async_remote_copy(
            src_ref=stat_all.at[dp],
            dst_ref=stat_all.at[dp],
            send_sem=all_ssem.at[step],
            recv_sem=all_rsem.at[step],
            device_id={"dp": lax.rem(dp + step, groups)},
            device_id_type=MESH,
        )

    for step in range(1, groups):
        all_copy(step).start()
    for step in range(2, lines):
        relay(order[-1], step)

    for turn in turns:
        turn.wait_recv()
    turned_all[dp] = turned[pl.ds(pl.multiple_of(dp * block, block), block), :]
    for c in order:
        for o in range(lines):
            x_copy(c, 2 * o + 1 - inner).wait_recv()

    result = jnp.zeros((block, 2 * feat), F32)
    for g in range(groups):
        for c in range(CHUNKS):
            result = result + dot(turned_all[g, :, c * rows : (c + 1) * rows], gathered[c, g])
    signs = pattern[pl.ds(pl.multiple_of(dp * block, block), block), :].astype(F32) * (1.0 / groups)
    diag_query[...] = result[:, :feat] * signs
    diag_key[...] = result[:, feat:] * signs
    for step in range(1, groups):
        all_copy(step).wait_recv()
    mean_out[...] = jnp.sum(stat_all[...], axis=0) * (1.0 / groups) / entries

    for turn in turns:
        turn.wait_send()
    for c in order:
        pair_copy(c).wait_send()
        chip_copy(c).wait_send()
        res_copy(c, kind).wait_send()
        for step in range(0, lines):
            @pl.when((outer - step >= 0) & (outer + 1 < lines))
            def _():
                line_copy(c, dp - 2 * step, dp + 2, 0).wait_send()

            @pl.when((outer + step < lines) & (outer >= 1))
            def _():
                line_copy(c, dp + 2 * step, dp - 2, 1).wait_send()

        for o in range(lines):
            x_copy(c, 2 * o + inner).wait_send()
    stat_copy(0, pair).wait_send()
    stat_copy(1, chip).wait_send()
    for step in range(1, groups):
        all_copy(step).wait_send()


def local(
    tokens,
    targets,
    loss_weights,
    segments,
    probe_model,
    probe_heads,
    norm_gain,
    w_query,
    w_key,
    w_value,
    w_out,
):
    groups = lax.axis_size("dp")
    parts = lax.axis_size("mp")
    assert parts == 4 and groups % 2 == 0
    seq, width = tokens.shape
    feat = w_query.shape[1]
    heads = feat // HEAD_DIM
    block = width // groups
    rows = seq // CHUNKS
    position = jnp.arange(seq, dtype=jnp.int32).astype(F32)
    exponent = jnp.arange(0, HEAD_DIM, 2, dtype=jnp.int32).astype(F32) / HEAD_DIM
    angles = position[:, None] * (10000.0 ** (-exponent))[None, :]
    cos, sin = jnp.cos(angles), jnp.sin(angles)
    cosine = jnp.concatenate([cos, cos], axis=1)
    sine = jnp.concatenate([-sin, sin], axis=1)
    vmem = pl.BlockSpec(memory_space=pltpu.VMEM)
    anywhere = pl.BlockSpec(memory_space=pl.ANY)
    dma = pltpu.SemaphoreType.DMA
    diag_query, diag_key, means = pl.pallas_call(
        functools.partial(kernel, groups, parts, float(width * feat * parts)),
        out_shape=(
            jax.ShapeDtypeStruct((block, feat), F32),
            jax.ShapeDtypeStruct((block, feat), F32),
            jax.ShapeDtypeStruct((1, HEAD_DIM), F32),
        ),
        in_specs=[vmem] * 10 + [anywhere] * 4,
        out_specs=(vmem, vmem, vmem),
        scratch_shapes=[
            pltpu.VMEM((width, feat), BF16),
            pltpu.VMEM((width, feat), BF16),
            pltpu.VMEM((width, feat), BF16),
            pltpu.VMEM((feat, width), BF16),
            pltpu.VMEM((seq, width), BF16),
            pltpu.VMEM((seq, width), BF16),
            pltpu.VMEM((width, seq), BF16),
            pltpu.VMEM((groups, block, seq), BF16),
            pltpu.VMEM((width, feat), BF16),
            pltpu.VMEM((seq, feat), F32),
            pltpu.VMEM((seq, feat), F32),
            pltpu.VMEM((seq, feat), F32),
            pltpu.VMEM((seq, feat), F32),
            pltpu.VMEM((heads, seq, seq), F32),
            pltpu.VMEM((heads, seq, seq), F32),
            pltpu.VMEM((2, seq, feat), BF16),
            pltpu.VMEM((seq, width), BF16),
            pltpu.VMEM((seq, width), F32),
            pltpu.VMEM((seq, width), BF16),
            pltpu.VMEM((seq, width), BF16),
            pltpu.VMEM((seq, width), BF16),
            pltpu.VMEM((2, seq, width), BF16),
            pltpu.VMEM((seq, feat), F32),
            pltpu.VMEM((CHUNKS, groups, rows, 2 * feat), BF16),
            pltpu.VMEM((2, 1, HEAD_DIM), F32),
            pltpu.VMEM((2, 1, HEAD_DIM), F32),
            pltpu.VMEM((groups, 1, HEAD_DIM), F32),
            dma((4,)),
            dma((groups,)),
            dma((groups,)),
            dma((CHUNKS,)),
            dma((CHUNKS,)),
            dma((CHUNKS,)),
            dma((CHUNKS,)),
            dma((CHUNKS,)),
            dma((CHUNKS,)),
            dma((CHUNKS, 2, groups)),
            dma((CHUNKS, groups)),
            dma((CHUNKS, groups)),
            dma((2,)),
            dma((2,)),
            dma((groups,)),
            dma((groups,)),
        ],
        compiler_params=pltpu.CompilerParams(
            collective_id=0, has_side_effects=True, vmem_limit_bytes=63 * 1024 * 1024
        ),
    )(
        tokens,
        targets,
        (loss_weights / seq)[:, None],
        segments.reshape(seq, 1),
        segments.reshape(1, seq),
        2.0 * probe_model.astype(F32) - 1.0,
        2.0 * probe_heads[0].astype(F32) - 1.0,
        norm_gain[None, :],
        cosine,
        sine,
        w_query,
        w_key,
        w_value,
        w_out,
    )
    mean_diag = jnp.stack([means[0, 0], means[0, HEAD_DIM // 2]])
    return (diag_query, diag_key, mean_diag)


def solution(mesh):
    placed = (
        P("dp", None),
        P("dp", None),
        P("dp"),
        P("dp", None),
        P("dp", None),
        P("dp", None, "mp"),
        P(),
        P(None, "mp"),
        P(None, "mp"),
        P(None, "mp"),
        P("mp", None),
    )
    return jax.shard_map(
        local,
        mesh=mesh,
        in_specs=placed,
        out_specs=(P("dp", "mp"), P("dp", "mp"), P()),
        check_vma=False,
    )
```

profile of v0, /device:TPU:0, one launch (start us, length us, event | category | flops | bytes accessed | tf_op | source)
XLA Modules:
  0.0 105.6 jit_solution(14301916300169370918)
XLA Ops:
  0.6 0.7 broadcast_multiply_fusion
  1.3 1.3 %add_bitcast_fusion.head_sign = f32[2,512]{1,0:T(2,128)} fusion(s32[1,2,512]{2,1,0:T(2,128)} %param.16), kind=kLoop, calls=%fused_computation.6 | loop fusion | flops 3072 | bytes 8192 | tf_op jit(solution)/shard_map/sub | solution.py:553
  2.6 1.3 %multiply_add_fusion.model_sign = f32[1,2048]{1,0:T(1,128)} fusion(s32[1,2048]{1,0:T(1,128)} %param.15), kind=kLoop, calls=%fused_computation.5 | loop fusion | flops 6144 | bytes 16384 | tf_op jit(solution)/shard_map/sub | solution.py:552
  3.9 0.8 copy.14.row_weights
  4.7 1.5 %copy.15.seg_col = s32[256,1]{1,0:T(8,128)} copy(s32[256,1]{0,1:T(1,128)} %bitcast.9) | data formatting | bytes 2048 | tf_op jit(solution)/shard_map/reshape | solution.py:550
  6.2 0.5 fusion
  6.7 0.8 pad_maximum_fusion
  7.6 91.2 %shard_map.130 = (f32[256,512]{1,0:T(8,128)}, f32[256,512]{1,0:T(8,128)}, f32[1,128]{1,0:T(1,128)}) custom-call(bf16[256,2048]{1,0:T(8,128)(2,1)} %tokens.1, bf16[256,2048]{1,0:T(8,128)(2,1)} %targets.1, f32[256,1]{1,0:T(8,128)} %copy.14.row_weights, s32[256,1]{1,0:T(8,128)} %copy.15.seg_col, s32[1,256]{1,0:T(1,128)} %seg_row.1, ...), custom_call_target="tpu_custom_call" | custom-call | tf_op jit(solution)/shard_map/pallas_call | solution.py:489
  98.7 1.2 %fusion.1 = (f32[1,1]{1,0:T(1,128)}, f32[1,1]{1,0:T(1,128)}) fusion(f32[1,128]{1,0:T(1,128)} %get-tuple-element.8), kind=kLoop, calls=%fused_computation.11 | loop fusion | bytes 16 | tf_op jit(solution)/shard_map/slice | solution.py:562
  100.0 1.9 %pad_maximum_fusion.2 = f32[2]{0:T(128)} fusion(f32[1]{0:T(128)} %bitcast.5, f32[1]{0:T(128)} %bitcast.4), kind=kLoop, calls=%fused_computation.8 | loop fusion | flops 2 | bytes 16 | tf_op jit(solution)/shard_map/stack | solution.py:562
  101.9 1.9 %copy.18 = f32[256,512]{1,0:T(8,128)} copy(f32[256,512]{1,0:T(8,128)} %get-tuple-element.19) | data formatting | bytes 1048576
  103.7 1.9 %copy.19 = f32[256,512]{1,0:T(8,128)} copy(f32[256,512]{1,0:T(8,128)} %get-tuple-element.20) | data formatting | bytes 1048576
  (2 shorter events, 0.0 us)
where the time goes:
time: 106 us
  Pallas kernels  91.2 us (86%)
  local copies, waits for them, and re-layouts  7.24 us (7%)
  other arithmetic  6.52 us (6%)
    pallas_call x1, Pallas kernels, local(): pl.pallas_call(functools.partial(kernel, groups, parts, float(width * fea...  91.2 us
    unnamed x2, local copies, waits for them, and re-layouts  3.73 us

commit v1 on v0

v1 whole, which is shorter than its diff:
```python
import functools

import jax
import jax.numpy as jnp
import numpy as np
from jax import lax
from jax.experimental import pallas as pl
from jax.experimental.pallas import tpu as pltpu
from jax.sharding import PartitionSpec as P

HEAD_DIM = 128
PAIR = 2 * HEAD_DIM
PRIME = 32749
F32 = jnp.float32
BF16 = jnp.bfloat16
MESH = pl.DeviceIdType.MESH

NN = (((1,), (0,)), ((), ()))
NT = (((1,), (1,)), ((), ()))
TN = (((0,), (0,)), ((), ()))


def dot(left, right, dims=NN):
    return lax.dot_general(left, right, dims, preferred_element_type=F32)


def low(left, right, dims=NN):
    return dot(left.astype(BF16), right.astype(BF16), dims)


def halves(array):
    high = array.astype(BF16)
    return high, (array - high.astype(F32)).astype(BF16)


def residue(whole):
    value = whole.astype(F32)
    left = value - jnp.floor(value * (1.0 / PRIME)) * PRIME
    left = jnp.where(left < 0, left + PRIME, left)
    left = jnp.where(left >= PRIME, left - PRIME, left)
    return left.astype(jnp.int32)


def pattern_block(row_part, col_part):
    mixed = row_part + col_part
    mixed = jnp.where(mixed >= PRIME, mixed - PRIME, mixed)
    square = mixed * mixed
    times = (square.astype(F32) * (1.0 / PRIME)).astype(jnp.int32)
    left = square - times * PRIME
    left = jnp.where(left < 0, left + PRIME, left)
    left = jnp.where(left >= PRIME, left - PRIME, left)
    odd = jnp.bitwise_and(jnp.right_shift(left * 52429, 18), 1)
    return jnp.where(odd == 1, -1.0, 1.0).astype(BF16)


def rotate(array, cos, sin):
    return array * cos + pltpu.roll(array, HEAD_DIM // 2, 1) * sin


def unrotate(array, cos, sin):
    return array * cos - pltpu.roll(array, HEAD_DIM // 2, 1) * sin


def kernel(
    groups,
    parts,
    entries,
    chunks,
    weights_row,
    seg_row,
    model_bits,
    head_bits,
    gain,
    cosine,
    sine,
    tokens_hbm,
    targets_hbm,
    wq_hbm,
    wk_hbm,
    wv_hbm,
    wo_hbm,
    diag_query,
    diag_key,
    mean_out,
    tokens,
    targets,
    wq,
    wk,
    wv,
    wo,
    wo_turned,
    normed,
    signed,
    slabs,
    slabs_turned,
    pattern,
    product,
    left_main,
    left_rest,
    right_main,
    right_rest,
    values,
    soft,
    d_soft,
    attended,
    out_send,
    own_part,
    pair_recv,
    chip_send,
    chip_recv,
    residual,
    hk_sum,
    gathered,
    x_send,
    x_recv,
    own_sum,
    result,
    stat_send,
    stat_recv,
    stat_all,
    load_sem,
    slab_ssem,
    slab_rsem,
    share_ssem,
    share_rsem,
    pair_ssem,
    pair_rsem,
    chip_ssem,
    chip_rsem,
    res_ssem,
    res_rsem,
    line_ssem,
    line_rsem,
    x_ssem,
    x_rsem,
    stat_ssem,
    stat_rsem,
    all_ssem,
    all_rsem,
    out_sem,
):
    seq, width = tokens.shape
    feat = wq.shape[1]
    heads = feat // HEAD_DIM
    block = width // groups
    lines = groups // 2
    slab = 2 * block
    half = seq // 2
    count = len(chunks)
    dp = lax.axis_index("dp")
    mp = lax.axis_index("mp")
    kind = lax.rem(mp, 2)
    other = 1 - kind
    pair = mp + 1 - 2 * kind
    chip = lax.rem(mp + 2, parts)
    inner = lax.rem(dp, 2)
    outer = dp // 2
    x_peer = dp + 1 - 2 * inner

    loads = []
    for n, (source, target) in enumerate(
        (
            (tokens_hbm, tokens),
            (wq_hbm, wq),
            (wk_hbm, wk),
            (wv_hbm, wv),
            (wo_hbm, wo),
            (targets_hbm, targets),
        )
    ):
        load = pltpu.make_async_copy(source, target, load_sem.at[n])
        load.start()
        loads.append(load)

    barrier = pltpu.get_barrier_semaphore()
    for step in range(1, lines):
        peer = lax.rem(outer + step, lines) * 2 + inner
        pl.semaphore_signal(barrier, inc=1, device_id={"dp": peer}, device_id_type=MESH)
    pl.semaphore_signal(barrier, inc=1, device_id={"dp": x_peer}, device_id_type=MESH)
    pl.semaphore_signal(barrier, inc=1, device_id={"mp": pair}, device_id_type=MESH)
    pl.semaphore_signal(barrier, inc=1, device_id={"mp": chip}, device_id_type=MESH)

    col_part = residue((mp * feat + lax.broadcasted_iota(jnp.int32, (1, feat), 1)) * 2713)
    for start in range(0, width, 256):
        row_part = residue((start + lax.broadcasted_iota(jnp.int32, (256, 1), 0)) * 1103 + 7)
        pattern[start : start + 256, :] = pattern_block(row_part, col_part)

    model_sign = 2.0 * model_bits[...].astype(F32) - 1.0
    head_sign = 2.0 * head_bits[0].astype(F32) - 1.0
    loads[0].wait()
    token_float = tokens[...].astype(F32)
    inverse = lax.rsqrt(jnp.sum(token_float * token_float, axis=1, keepdims=True) / width + 1e-06)
    for start in range(0, width, 256):
        cols = slice(start, start + 256)
        part = (tokens[:, cols].astype(F32) * inverse * gain[:, cols]).astype(BF16)
        normed[:, cols] = part
        signed[:, cols] = (part.astype(F32) * model_sign[:, cols]).astype(BF16)

    pl.semaphore_wait(barrier, lines + 2)

    def slab_copy(step):
        peer = lax.rem(outer + step, lines)
        return pltpu.make_async_remote_copy(
            src_ref=signed.at[
                pl.ds(pl.multiple_of(kind * half, half), half),
                pl.ds(pl.multiple_of(peer * slab, slab), slab),
            ],
            dst_ref=slabs.at[outer, pl.ds(pl.multiple_of(kind * half, half), half), :],
            send_sem=slab_ssem.at[step],
            recv_sem=slab_rsem.at[step],
            device_id={"dp": peer * 2 + inner},
            device_id_type=MESH,
        )

    def share_copy(step):
        owner = lax.rem(outer - step + lines, lines)
        mine = slabs.at[owner, pl.ds(pl.multiple_of(kind * half, half), half), :]
        return pltpu.make_async_remote_copy(
            src_ref=mine,
            dst_ref=mine,
            send_sem=share_ssem.at[step],
            recv_sem=share_rsem.at[step],
            device_id={"mp": pair},
            device_id_type=MESH,
        )

    for step in range(1, lines):
        slab_copy(step).start()

    cos = cosine[...]
    sin = sine[...]
    scale = HEAD_DIM ** (-0.5)

    loads[1].wait()
    query = dot(normed[...], wq[...])
    for h in range(heads):
        cols = slice(h * HEAD_DIM, (h + 1) * HEAD_DIM)
        high, rest = halves(rotate(query[:, cols], cos, sin))
        left_main[h, :, HEAD_DIM:] = high
        left_rest[h, :, HEAD_DIM:] = rest
    loads[2].wait()
    keys = dot(normed[...], wk[...])
    for h in range(heads):
        cols = slice(h * HEAD_DIM, (h + 1) * HEAD_DIM)
        high, rest = halves(rotate(keys[:, cols], cos, sin))
        right_main[h, :, :HEAD_DIM] = high
        right_rest[h, :, :HEAD_DIM] = rest
    product[...] = dot(signed[...], pattern[...])
    for h in range(heads):
        cols = slice(h * HEAD_DIM, (h + 1) * HEAD_DIM)
        probe = product[:, cols]
        high, rest = halves(rotate(probe * head_sign[0:1, cols], cos, sin))
        left_main[h, :, :HEAD_DIM] = high
        left_rest[h, :, :HEAD_DIM] = rest
        high, rest = halves(rotate(probe * head_sign[1:2, cols], cos, sin))
        right_main[h, :, HEAD_DIM:] = high
        right_rest[h, :, HEAD_DIM:] = rest
    loads[3].wait()
    values[...] = dot(normed[...], wv[...]).astype(BF16)

    place_q = lax.broadcasted_iota(jnp.int32, (seq, seq), 0)
    place_k = lax.broadcasted_iota(jnp.int32, (seq, seq), 1)
    same = place_q == place_k
    segments = seg_row[...].astype(F32)
    seg_col = jnp.sum(jnp.where(same, segments, 0.0), axis=1, keepdims=True)
    row_weights = jnp.sum(jnp.where(same, weights_row[...], 0.0), axis=1, keepdims=True) / seq

    def pair_copy(c):
        first, rows = chunks[c]
        return pltpu.make_async_remote_copy(
            src_ref=out_send.at[pl.ds(first, rows), :],
            dst_ref=pair_recv.at[pl.ds(first, rows), :],
            send_sem=pair_ssem.at[c],
            recv_sem=pair_rsem.at[c],
            device_id={"mp": pair},
            device_id_type=MESH,
        )

    def chip_copy(c):
        first, rows = chunks[c]
        return pltpu.make_async_remote_copy(
            src_ref=chip_send.at[pl.ds(first, rows), :],
            dst_ref=chip_recv.at[pl.ds(first, rows), :],
            send_sem=chip_ssem.at[c],
            recv_sem=chip_rsem.at[c],
            device_id={"mp": chip},
            device_id_type=MESH,
        )

    def res_copy(c, which):
        first, rows = chunks[c]
        return pltpu.make_async_remote_copy(
            src_ref=residual.at[which, pl.ds(first, rows), :],
            dst_ref=residual.at[which, pl.ds(first, rows), :],
            send_sem=res_ssem.at[c],
            recv_sem=res_rsem.at[c],
            device_id={"mp": pair},
            device_id_type=MESH,
        )

    def attend(c):
        first, rows = chunks[c]
        reach = first + rows
        span = slice(first, reach)
        allowed = (
            (first + lax.broadcasted_iota(jnp.int32, (rows, reach), 0))
            >= lax.broadcasted_iota(jnp.int32, (rows, reach), 1)
        ) & (seg_col[span, :] == segments[:, :reach])
        for h in range(heads):
            cols = slice(h * HEAD_DIM, (h + 1) * HEAD_DIM)
            both = left_main[h, span, :]
            rest = left_rest[h, span, :]
            main_k = right_main[h, :reach, :]
            rest_k = right_rest[h, :reach, :]
            q = both[:, HEAD_DIM:]
            k = main_k[:, :HEAD_DIM]
            scores = (
                dot(q, k, NT)
                + dot(rest[:, HEAD_DIM:], k, NT)
                + dot(q, rest_k[:, :HEAD_DIM], NT)
            ) * scale
            d_scores = (dot(both, main_k, NT) + dot(rest, main_k, NT) + dot(both, rest_k, NT)) * scale
            raised = jnp.where(allowed, jnp.exp(scores), 0.0)
            p = raised / jnp.sum(raised, axis=1, keepdims=True)
            d_p = p * (d_scores - jnp.sum(p * d_scores, axis=1, keepdims=True))
            soft[h, span, :reach] = p
            d_soft[h, span, :reach] = d_p
            v = values[:reach, cols]
            attended[0, span, cols] = low(p, v).astype(BF16)
            attended[1, span, cols] = low(d_p, v).astype(BF16)

    def project(c):
        first, rows = chunks[c]
        span = slice(first, first + rows)
        out_send[span, :] = dot(attended[other, span, :], wo[...]).astype(BF16)
        pair_copy(c).start()
        own_part[span, :] = dot(attended[kind, span, :], wo[...])
        pair_copy(c).wait_recv()
        summed = own_part[span, :] + pair_recv[span, :].astype(F32)
        own_part[span, :] = summed
        chip_send[span, :] = summed.astype(BF16)
        chip_copy(c).start()

    def line_copy(c, h, slot, target, way):
        first, rows = chunks[c]
        here = gathered.at[h, slot, pl.ds(first, rows), :]
        return pltpu.make_async_remote_copy(
            src_ref=here,
            dst_ref=here,
            send_sem=line_ssem.at[c, h, way],
            recv_sem=line_rsem.at[c, h, slot],
            device_id={"dp": target * 2 + inner},
            device_id_type=MESH,
        )

    def line_wait(c, h, slot):
        line_copy(c, h, slot, outer, 0).wait_recv()

    def own_sends(c, h, act):
        for way, hop in enumerate((2, -2, 1, -1)):
            @pl.when((outer + hop >= 0) & (outer + hop < lines))
            def _():
                act(line_copy(c, h, outer, outer + hop, way))

    def relays(c, h, step, side, act, arrive):
        slot = outer - side * 2 * step
        for n in range(2):
            hop = side * (n + 1)

            @pl.when((slot >= 0) & (slot < lines) & (outer + hop >= 0) & (outer + hop < lines))
            def _():
                if arrive and n == 0:
                    line_wait(c, h, slot)
                act(line_copy(c, h, slot, outer + hop, 4 * step + (side + 1) + n))

    def relay(c, h):
        for step in range(1, (lines + 1) // 2):
            for side in (1, -1):
                relays(c, h, step, side, lambda copy: copy.start(), True)

    def arrive(c, h):
        for slot in range(lines):
            gap = outer - slot
            far = gap if isinstance(gap, int) else jnp.abs(gap)
            onward = jnp.where(gap > 0, outer + 1 < lines, outer >= 1)
            passed = (lax.rem(far, 2) == 0) & onward

            @pl.when((far > 0) & jnp.logical_not(passed))
            def _():
                line_wait(c, h, slot)

    wanted = jnp.where(kind == 0, 1.0, 0.0)
    sums = [jnp.zeros((1, HEAD_DIM), F32), jnp.zeros((1, HEAD_DIM), F32)]

    def curve(c):
        first, rows = chunks[c]
        reach = first + rows
        span = slice(first, reach)
        chip_copy(c).wait_recv()
        whole = own_part[span, :] + chip_recv[span, :].astype(F32)
        shift = tokens[span, :].astype(F32) - targets[span, :].astype(F32)
        residual[kind, span, :] = ((whole + wanted * shift) * row_weights[span, :]).astype(BF16)
        res_copy(c, kind).start()
        back_own = dot(residual[kind, span, :], wo_turned[...])
        res_copy(c, other).wait_recv()
        back_other = dot(residual[other, span, :], wo_turned[...])
        back = jnp.where(kind == 0, back_own, back_other).astype(BF16)
        back_tangent = jnp.where(kind == 0, back_other, back_own).astype(BF16)
        cos_q = cos[span, :]
        sin_q = sin[span, :]
        for h in range(heads):
            cols = slice(h * HEAD_DIM, (h + 1) * HEAD_DIM)
            left = left_main[h, span, :]
            right = right_main[h, :reach, :]
            v = values[:reach, cols]
            p = soft[h, span, :reach]
            d_p = d_soft[h, span, :reach]
            u = dot(back[:, cols], v, NT)
            u_tangent = dot(back_tangent[:, cols], v, NT)
            centered = u - jnp.sum(p * u, axis=1, keepdims=True)
            level = jnp.sum(d_p * u + p * u_tangent, axis=1, keepdims=True)
            mixed = ((d_p * centered + p * (u_tangent - level)) * scale).astype(BF16)
            lead = (p * centered * scale).astype(BF16)
            hq = dot(mixed, right[:, :HEAD_DIM]) + dot(lead, right[:, HEAD_DIM:])
            hk = dot(mixed, left[:, HEAD_DIM:], TN) + dot(lead, left[:, :HEAD_DIM], TN)
            if c > 0:
                hk = hk_sum[:reach, cols] + hk
            if c < count - 1:
                hk_sum[:reach, cols] = hk
            hq = unrotate(hq, cos_q, sin_q)
            hk = unrotate(hk[span, :], cos_q, sin_q)
            hq = (hq.astype(BF16).astype(F32) * head_sign[0:1, cols]).astype(BF16)
            hk = (hk.astype(BF16).astype(F32) * head_sign[1:2, cols]).astype(BF16)
            gathered[h, outer, span, :HEAD_DIM] = hq
            gathered[h, outer, span, HEAD_DIM:] = hk
            own_sends(c, h, lambda copy: copy.start())
            probe = product[span, cols]
            sums[0] = sums[0] + jnp.sum(hq.astype(F32) * probe, axis=0, keepdims=True)
            sums[1] = sums[1] + jnp.sum(hk.astype(F32) * probe, axis=0, keepdims=True)

    attend(0)
    loads[4].wait()
    project(0)
    for c in range(1, count):
        attend(c)
        project(c)
    loads[5].wait()
    wo_turned[...] = jnp.transpose(wo[...])
    for step in range(1, lines):
        slab_copy(step).wait_recv()
        share_copy(step).start()
    slabs[outer] = signed[:, pl.ds(pl.multiple_of(outer * slab, slab), slab)]

    curve(0)
    for step in range(1, lines):
        share_copy(step).wait_recv()
    for o in range(lines):
        slabs_turned[:, o * seq : (o + 1) * seq] = jnp.transpose(slabs[o])
    for c in range(1, count):
        curve(c)
        for h in range(heads):
            relay(c - 1, h)

    lane = lax.broadcasted_iota(jnp.int32, (1, HEAD_DIM), 1)
    stat_send[0] = jnp.where(
        lane < HEAD_DIM // 2,
        jnp.sum(sums[0], axis=1, keepdims=True),
        jnp.sum(sums[1], axis=1, keepdims=True),
    )

    def stat_copy(n):
        target = ({"mp": pair}, {"mp": chip}, {"dp": x_peer})[n]
        return pltpu.make_async_remote_copy(
            src_ref=stat_send.at[n],
            dst_ref=stat_recv.at[n],
            send_sem=stat_ssem.at[n],
            recv_sem=stat_rsem.at[n],
            device_id=target,
            device_id_type=MESH,
        )

    def all_copy(step):
        return pltpu.make_async_remote_copy(
            src_ref=stat_all.at[outer],
            dst_ref=stat_all.at[outer],
            send_sem=all_ssem.at[step],
            recv_sem=all_rsem.at[step],
            device_id={"dp": lax.rem(outer + step, lines) * 2 + inner},
            device_id_type=MESH,
        )

    def x_copy(h):
        return pltpu.make_async_remote_copy(
            src_ref=x_send.at[h],
            dst_ref=x_recv.at[h],
            send_sem=x_ssem.at[h],
            recv_sem=x_rsem.at[h],
            device_id={"dp": x_peer},
            device_id_type=MESH,
        )

    stat_copy(0).start()
    own_rows = pl.ds(pl.multiple_of(inner * block, block), block)
    peer_rows = pl.ds(pl.multiple_of((1 - inner) * block, block), block)
    for h in range(heads):
        relay(count - 1, h)
        if h < 3:
            stat_copy(h).wait_recv()
            total = stat_send[h] + stat_recv[h]
            if h < 2:
                stat_send[h + 1] = total
                stat_copy(h + 1).start()
            else:
                stat_all[outer] = total
                for step in range(1, lines):
                    all_copy(step).start()
    for h in range(heads):
        for c in range(count):
            arrive(c, h)
        stack = gathered[h].reshape(lines * seq, PAIR)
        x_send[h] = dot(slabs_turned[peer_rows, :], stack).astype(BF16)
        x_copy(h).start()
        own_sum[h] = dot(slabs_turned[own_rows, :], stack)

    def out_copies(h):
        cols = pl.ds(h * HEAD_DIM, HEAD_DIM)
        return [
            pltpu.make_async_copy(result.at[n, :, cols], target.at[:, cols], out_sem.at[n, h])
            for n, target in enumerate((diag_query, diag_key))
        ]

    for h in range(heads):
        cols = slice(h * HEAD_DIM, (h + 1) * HEAD_DIM)
        signs = pattern[pl.ds(pl.multiple_of(dp * block, block), block), cols].astype(F32) * (1.0 / groups)
        x_copy(h).wait_recv()
        total = own_sum[h] + x_recv[h].astype(F32)
        result[0, :, cols] = total[:, :HEAD_DIM] * signs
        result[1, :, cols] = total[:, HEAD_DIM:] * signs
        for copy in out_copies(h):
            copy.start()
    for step in range(1, lines):
        all_copy(step).wait_recv()
    mean_out[...] = jnp.sum(stat_all[...], axis=0) * (1.0 / groups) / entries

    for step in range(1, lines):
        slab_copy(step).wait_send()
        share_copy(step).wait_send()
        all_copy(step).wait_send()
    for c in range(count):
        pair_copy(c).wait_send()
        chip_copy(c).wait_send()
        res_copy(c, kind).wait_send()
        for h in range(heads):
            own_sends(c, h, lambda copy: copy.wait_send())
            for step in range(1, (lines + 1) // 2):
                for side in (1, -1):
                    relays(c, h, step, side, lambda copy: copy.wait_send(), False)
    for n in range(3):
        stat_copy(n).wait_send()
    for h in range(heads):
        x_copy(h).wait_send()
        for copy in out_copies(h):
            copy.wait()


def local(
    tokens,
    targets,
    loss_weights,
    segments,
    probe_model,
    probe_heads,
    norm_gain,
    w_query,
    w_key,
    w_value,
    w_out,
):
    groups = lax.axis_size("dp")
    parts = lax.axis_size("mp")
    assert parts == 4 and groups % 2 == 0
    seq, width = tokens.shape
    feat = w_query.shape[1]
    heads = feat // HEAD_DIM
    block = width // groups
    lines = groups // 2
    quarter = seq // 4
    chunks = ((3 * quarter, quarter), (2 * quarter, quarter), (0, 2 * quarter))
    count = len(chunks)
    position = np.arange(seq, dtype=np.float32)
    exponent = np.arange(0, HEAD_DIM, 2).astype(np.float32) / np.float32(HEAD_DIM)
    angles = position[:, None] * (np.float32(10000.0) ** (-exponent)).astype(np.float32)[None, :]
    cos = np.cos(angles.astype(np.float64)).astype(np.float32)
    sin = np.sin(angles.astype(np.float64)).astype(np.float32)
    cosine = np.concatenate([cos, cos], axis=1)
    sine = np.concatenate([-sin, sin], axis=1)
    vmem = pl.BlockSpec(memory_space=pltpu.VMEM)
    anywhere = pl.BlockSpec(memory_space=pl.ANY)
    dma = pltpu.SemaphoreType.DMA
    ways = 4 + 4 * ((lines + 1) // 2 - 1) + 4
    diag_query, diag_key, means = pl.pallas_call(
        functools.partial(kernel, groups, parts, float(width * feat * parts), chunks),
        out_shape=(
            jax.ShapeDtypeStruct((block, feat), F32),
            jax.ShapeDtypeStruct((block, feat), F32),
            jax.ShapeDtypeStruct((1, HEAD_DIM), F32),
        ),
        in_specs=[vmem] * 7 + [anywhere] * 6,
        out_specs=(anywhere, anywhere, vmem),
        scratch_shapes=[
            pltpu.VMEM((seq, width), BF16),
            pltpu.VMEM((seq, width), BF16),
            pltpu.VMEM((width, feat), BF16),
            pltpu.VMEM((width, feat), BF16),
            pltpu.VMEM((width, feat), BF16),
            pltpu.VMEM((feat, width), BF16),
            pltpu.VMEM((width, feat), BF16),
            pltpu.VMEM((seq, width), BF16),
            pltpu.VMEM((seq, width), BF16),
            pltpu.VMEM((lines, seq, 2 * block), BF16),
            pltpu.VMEM((2 * block, lines * seq), BF16),
            pltpu.VMEM((width, feat), BF16),
            pltpu.VMEM((seq, feat), F32),
            pltpu.VMEM((heads, seq, PAIR), BF16),
            pltpu.VMEM((heads, seq, PAIR), BF16),
            pltpu.VMEM((heads, seq, PAIR), BF16),
            pltpu.VMEM((heads, seq, PAIR), BF16),
            pltpu.VMEM((seq, feat), BF16),
            pltpu.VMEM((heads, seq, seq), F32),
            pltpu.VMEM((heads, seq, seq), F32),
            pltpu.VMEM((2, seq, feat), BF16),
            pltpu.VMEM((seq, width), BF16),
            pltpu.VMEM((seq, width), F32),
            pltpu.VMEM((seq, width), BF16),
            pltpu.VMEM((seq, width), BF16),
            pltpu.VMEM((seq, width), BF16),
            pltpu.VMEM((2, seq, width), BF16),
            pltpu.VMEM((seq, feat), F32),
            pltpu.VMEM((heads, lines, seq, PAIR), BF16),
            pltpu.VMEM((heads, block, PAIR), BF16),
            pltpu.VMEM((heads, block, PAIR), BF16),
            pltpu.VMEM((heads, block, PAIR), F32),
            pltpu.VMEM((2, block, feat), F32),
            pltpu.VMEM((3, 1, HEAD_DIM), F32),
            pltpu.VMEM((3, 1, HEAD_DIM), F32),
            pltpu.VMEM((lines, 1, HEAD_DIM), F32),
            dma((6,)),
            dma((lines,)),
            dma((lines,)),
            dma((lines,)),
            dma((lines,)),
            dma((count,)),
            dma((count,)),
            dma((count,)),
            dma((count,)),
            dma((count,)),
            dma((count,)),
            dma((count, heads, ways)),
            dma((count, heads, lines)),
            dma((heads,)),
            dma((heads,)),
            dma((3,)),
            dma((3,)),
            dma((lines,)),
            dma((lines,)),
            dma((2, heads)),
        ],
        compiler_params=pltpu.CompilerParams(
            collective_id=0, has_side_effects=True, vmem_limit_bytes=58 * 1024 * 1024
        ),
    )(
        loss_weights.reshape(1, seq),
        segments,
        probe_model,
        probe_heads,
        norm_gain.reshape(1, width),
        jnp.asarray(cosine),
        jnp.asarray(sine),
        tokens,
        targets,
        w_query,
        w_key,
        w_value,
        w_out,
    )
    mean_diag = jnp.stack([means[0, 0], means[0, HEAD_DIM // 2]])
    return (diag_query, diag_key, mean_diag)


def solution(mesh):
    placed = (
        P("dp", None),
        P("dp", None),
        P("dp"),
        P("dp", None),
        P("dp", None),
        P("dp", None, "mp"),
        P(),
        P(None, "mp"),
        P(None, "mp"),
        P(None, "mp"),
        P("mp", None),
    )
    return jax.shard_map(
        local,
        mesh=mesh,
        in_specs=placed,
        out_specs=(P("dp", "mp"), P("dp", "mp"), P()),
        check_vma=False,
    )
```

time: 106 us -> 84.3 us (0.80)
  Pallas kernels: 91.2 us -> 76.5 us
  other arithmetic: 6.52 us -> 1.88 us
  local copies, waits for them, and re-layouts: 7.24 us -> 5.02 us
    pallas_call x1, Pallas kernels: 91.2 us -> 76.5 us  [local(): pl.pallas_call(functools.partial(kernel, groups, parts, float(width * fea...]
    sub x2 -> x0, other arithmetic: 2.58 us -> none  [the longest x1 1.29 us: local(): 2.0 * probe_model.astype(F32) - 1.0]
    reshape x1 -> x0, local copies, waits for them, and re-layouts: 1.47 us -> none  [local(): segments.reshape(seq, 1)]
where the time goes in v1:
time: 84.3 us; the launch traced here: 84 us
  Pallas kernels  76.5 us (91%)
  local copies, waits for them, and re-layouts  5.02 us (6%)
  other arithmetic  1.88 us (2%)
    pallas_call x1, Pallas kernels, local(): pl.pallas_call(functools.partial(kernel, groups, parts, float(width * fea...  76.5 us
    unnamed x2, local copies, waits for them, and re-layouts  3.73 us
    another operation x1, other arithmetic, local(): mean_diag = jnp.stack([means[0, 0], means[0, HEAD_DIM // 2]])  1.88 us

profile of v1, /device:TPU:0, one launch (start us, length us, event | category | flops | bytes accessed | tf_op | source)
XLA Modules:
  0.0 84.0 jit_solution(1940148896885743050)
XLA Ops:
  0.6 76.5 %shard_map.148 = (f32[256,512]{1,0:T(8,128)}, f32[256,512]{1,0:T(8,128)}, f32[1,128]{1,0:T(1,128)}) custom-call(f32[1,256]{1,0:T(1,128)} %bitcast.5, s32[1,256]{1,0:T(1,128)} %seg_row.1, s32[1,2048]{1,0:T(1,128)} %model_bits.1, s32[1,2,512]{2,1,0:T(2,128)} %head_bits.1, f32[1,2048]{1,0:T(1,128)} %bitcast.4, f32[256,128]{1,0:T(8,128)} %constant.4.clone.cosine, ...), custom_call_target="tpu_custom_call" | custom-call | tf_op jit(solution)/shard_map/pallas_call | solution.py:601
  77.1 1.3 %fusion = (f32[1,1]{1,0:T(1,128)}, f32[1,1]{1,0:T(1,128)}) fusion(f32[1,128]{1,0:T(1,128)} %get-tuple-element.8), kind=kLoop, calls=%fused_computation.1 | loop fusion | bytes 16 | tf_op jit(solution)/shard_map/slice | solution.py:686
  78.4 1.9 %pad_maximum_fusion = f32[2]{0:T(128)} fusion(f32[1]{0:T(128)} %bitcast.3, f32[1]{0:T(128)} %bitcast.2), kind=kLoop, calls=%fused_computation | loop fusion | flops 2 | bytes 16 | tf_op jit(solution)/shard_map/stack | solution.py:686
  80.3 1.9 %copy.18 = f32[256,512]{1,0:T(8,128)} copy(f32[256,512]{1,0:T(8,128)} %get-tuple-element.14) | data formatting | bytes 1048576
  82.1 1.9 %copy.19 = f32[256,512]{1,0:T(8,128)} copy(f32[256,512]{1,0:T(8,128)} %get-tuple-element.15) | data formatting | bytes 1048576

commit v2 on v1

--- a/solution.py
+++ b/solution.py
@@ -11,6 +11,7 @@
 HEAD_DIM = 128
 PAIR = 2 * HEAD_DIM
 PRIME = 32749
+SIZES = (2, 3, 5, 6)
 F32 = jnp.float32
 BF16 = jnp.bfloat16
 MESH = pl.DeviceIdType.MESH
@@ -33,24 +34,41 @@
     return high, (array - high.astype(F32)).astype(BF16)
 
 
-def residue(whole):
-    value = whole.astype(F32)
-    left = value - jnp.floor(value * (1.0 / PRIME)) * PRIME
+def modulo(whole):
+    times = (whole.astype(F32) * (1.0 / PRIME)).astype(jnp.int32)
+    left = whole - times * PRIME
     left = jnp.where(left < 0, left + PRIME, left)
-    left = jnp.where(left >= PRIME, left - PRIME, left)
-    return left.astype(jnp.int32)
-
-
-def pattern_block(row_part, col_part):
-    mixed = row_part + col_part
-    mixed = jnp.where(mixed >= PRIME, mixed - PRIME, mixed)
-    square = mixed * mixed
-    times = (square.astype(F32) * (1.0 / PRIME)).astype(jnp.int32)
-    left = square - times * PRIME
-    left = jnp.where(left < 0, left + PRIME, left)
-    left = jnp.where(left >= PRIME, left - PRIME, left)
-    odd = jnp.bitwise_and(jnp.right_shift(left * 52429, 18), 1)
-    return jnp.where(odd == 1, -1.0, 1.0).astype(BF16)
+    return jnp.where(left >= PRIME, left - PRIME, left)
+
+
+def wrap(value):
+    return jnp.where(value >= PRIME, value - PRIME, value)
+
+
+def fill_pattern(pattern, first_col, between):
+    step = 16
+    width, feat = pattern.shape
+    rows = lax.broadcasted_iota(jnp.int32, (step, 1), 0) * 1103 + 7
+    cols = modulo((first_col + lax.broadcasted_iota(jnp.int32, (1, feat), 1)) * 2713)
+    start = wrap(rows + cols)
+    jump = step * 1103 % PRIME
+    square = modulo(start * start).astype(F32)
+    change = modulo(start * (2 * jump) + jump * jump).astype(F32)
+    bend = float(2 * jump * jump % PRIME)
+    round_to = float(3 << 22)
+
+    def body(n, state):
+        square, change = state
+        tenth = square * 0.1 + 0.05
+        whole = (tenth + round_to) - round_to
+        signs = jnp.where(tenth >= whole, 1.0, -1.0)
+        pattern[pl.ds(pl.multiple_of(n * step, step), step), :] = signs.astype(BF16)
+        return wrap(square + change), wrap(change + bend)
+
+    middle = width // step // 2
+    state = lax.fori_loop(0, middle, body, (square, change), unroll=4)
+    between()
+    lax.fori_loop(middle, width // step, body, state, unroll=4)
 
 
 def rotate(array, cos, sin):
@@ -66,13 +84,13 @@
     parts,
     entries,
     chunks,
-    weights_row,
-    seg_row,
-    model_bits,
-    head_bits,
-    gain,
-    cosine,
-    sine,
+    weights_hbm,
+    seg_hbm,
+    model_hbm,
+    head_hbm,
+    gain_hbm,
+    cosine_hbm,
+    sine_hbm,
     tokens_hbm,
     targets_hbm,
     wq_hbm,
@@ -82,6 +100,13 @@
     diag_query,
     diag_key,
     mean_out,
+    weights_row,
+    seg_row,
+    model_bits,
+    head_bits,
+    gain,
+    cosine,
+    sine,
     tokens,
     targets,
     wq,
@@ -138,6 +163,7 @@
     all_ssem,
     all_rsem,
     out_sem,
+    small_sem,
 ):
     seq, width = tokens.shape
     feat = wq.shape[1]
@@ -168,9 +194,23 @@
             (targets_hbm, targets),
         )
     ):
-        load = pltpu.make_async_copy(source, target, load_sem.at[n])
-        load.start()
-        loads.append(load)
+        loads.append(pltpu.make_async_copy(source, target, load_sem.at[n]))
+    loads[0].start()
+    smalls = []
+    for n, (source, target) in enumerate(
+        (
+            (model_hbm, model_bits),
+            (gain_hbm, gain),
+            (head_hbm, head_bits),
+            (cosine_hbm, cosine),
+            (sine_hbm, sine),
+            (seg_hbm, seg_row),
+            (weights_hbm, weights_row),
+        )
+    ):
+        small = pltpu.make_async_copy(source, target, small_sem.at[n])
+        small.start()
+        smalls.append(small)
 
     barrier = pltpu.get_barrier_semaphore()
     for step in range(1, lines):
@@ -180,11 +220,14 @@
     pl.semaphore_signal(barrier, inc=1, device_id={"mp": pair}, device_id_type=MESH)
     pl.semaphore_signal(barrier, inc=1, device_id={"mp": chip}, device_id_type=MESH)
 
-    col_part = residue((mp * feat + lax.broadcasted_iota(jnp.int32, (1, feat), 1)) * 2713)
-    for start in range(0, width, 256):
-        row_part = residue((start + lax.broadcasted_iota(jnp.int32, (256, 1), 0)) * 1103 + 7)
-        pattern[start : start + 256, :] = pattern_block(row_part, col_part)
-
+    def load_more():
+        loads[1].start()
+        loads[2].start()
+
+    fill_pattern(pattern, mp * feat, load_more)
+
+    for small in smalls:
+        small.wait()
     model_sign = 2.0 * model_bits[...].astype(F32) - 1.0
     head_sign = 2.0 * head_bits[0].astype(F32) - 1.0
     loads[0].wait()
@@ -196,6 +239,8 @@
         normed[:, cols] = part
         signed[:, cols] = (part.astype(F32) * model_sign[:, cols]).astype(BF16)
 
+    for load in loads[3:]:
+        load.start()
     pl.semaphore_wait(barrier, lines + 2)
 
     def slab_copy(step):
@@ -231,6 +276,16 @@
     sin = sine[...]
     scale = HEAD_DIM ** (-0.5)
 
+    product[...] = dot(signed[...], pattern[...])
+    for h in range(heads):
+        cols = slice(h * HEAD_DIM, (h + 1) * HEAD_DIM)
+        probe = product[:, cols]
+        high, rest = halves(rotate(probe * head_sign[0:1, cols], cos, sin))
+        left_main[h, :, :HEAD_DIM] = high
+        left_rest[h, :, :HEAD_DIM] = rest
+        high, rest = halves(rotate(probe * head_sign[1:2, cols], cos, sin))
+        right_main[h, :, HEAD_DIM:] = high
+        right_rest[h, :, HEAD_DIM:] = rest
     loads[1].wait()
     query = dot(normed[...], wq[...])
     for h in range(heads):
@@ -245,16 +300,6 @@
         high, rest = halves(rotate(keys[:, cols], cos, sin))
         right_main[h, :, :HEAD_DIM] = high
         right_rest[h, :, :HEAD_DIM] = rest
-    product[...] = dot(signed[...], pattern[...])
-    for h in range(heads):
-        cols = slice(h * HEAD_DIM, (h + 1) * HEAD_DIM)
-        probe = product[:, cols]
-        high, rest = halves(rotate(probe * head_sign[0:1, cols], cos, sin))
-        left_main[h, :, :HEAD_DIM] = high
-        left_rest[h, :, :HEAD_DIM] = rest
-        high, rest = halves(rotate(probe * head_sign[1:2, cols], cos, sin))
-        right_main[h, :, HEAD_DIM:] = high
-        right_rest[h, :, HEAD_DIM:] = rest
     loads[3].wait()
     values[...] = dot(normed[...], wv[...]).astype(BF16)
 
@@ -302,32 +347,38 @@
         first, rows = chunks[c]
         reach = first + rows
         span = slice(first, reach)
-        allowed = (
-            (first + lax.broadcasted_iota(jnp.int32, (rows, reach), 0))
-            >= lax.broadcasted_iota(jnp.int32, (rows, reach), 1)
-        ) & (seg_col[span, :] == segments[:, :reach])
+        place = first + lax.broadcasted_iota(jnp.int32, (rows, reach), 0)
+        place = jnp.concatenate([place] * heads, axis=0)
+        owner = jnp.concatenate([seg_col[span, :]] * heads, axis=0)
+        allowed = (place >= lax.broadcasted_iota(jnp.int32, (heads * rows, reach), 1)) & (
+            owner == segments[:, :reach]
+        )
+        blank = jnp.zeros((rows, HEAD_DIM), BF16)
+        scores, d_scores = [], []
+        for h in range(heads):
+            both = left_main[h, span, :]
+            rest = left_rest[h, span, :]
+            q = jnp.concatenate([both[:, HEAD_DIM:], blank], axis=1)
+            q_rest = jnp.concatenate([rest[:, HEAD_DIM:], blank], axis=1)
+            main = dot(jnp.concatenate([both, rest, q, q_rest], axis=0), right_main[h, :reach, :], NT)
+            minor = dot(jnp.concatenate([both, q], axis=0), right_rest[h, :reach, :], NT)
+            d_scores.append(main[:rows] + (main[rows : 2 * rows] + minor[:rows]))
+            scores.append(main[2 * rows : 3 * rows] + (main[3 * rows :] + minor[rows:]))
+        scores = jnp.concatenate(scores, axis=0) * scale
+        d_scores = jnp.concatenate(d_scores, axis=0) * scale
+        raised = jnp.where(allowed, jnp.exp(scores), 0.0)
+        p = raised / jnp.sum(raised, axis=1, keepdims=True)
+        d_p = p * (d_scores - jnp.sum(p * d_scores, axis=1, keepdims=True))
+        soft[:, span, :reach] = p.reshape(heads, rows, reach)
+        d_soft[:, span, :reach] = d_p.reshape(heads, rows, reach)
+        p = p.astype(BF16)
+        d_p = d_p.astype(BF16)
         for h in range(heads):
             cols = slice(h * HEAD_DIM, (h + 1) * HEAD_DIM)
-            both = left_main[h, span, :]
-            rest = left_rest[h, span, :]
-            main_k = right_main[h, :reach, :]
-            rest_k = right_rest[h, :reach, :]
-            q = both[:, HEAD_DIM:]
-            k = main_k[:, :HEAD_DIM]
-            scores = (
-                dot(q, k, NT)
-                + dot(rest[:, HEAD_DIM:], k, NT)
-                + dot(q, rest_k[:, :HEAD_DIM], NT)
-            ) * scale
-            d_scores = (dot(both, main_k, NT) + dot(rest, main_k, NT) + dot(both, rest_k, NT)) * scale
-            raised = jnp.where(allowed, jnp.exp(scores), 0.0)
-            p = raised / jnp.sum(raised, axis=1, keepdims=True)
-            d_p = p * (d_scores - jnp.sum(p * d_scores, axis=1, keepdims=True))
-            soft[h, span, :reach] = p
-            d_soft[h, span, :reach] = d_p
-            v = values[:reach, cols]
-            attended[0, span, cols] = low(p, v).astype(BF16)
-            attended[1, span, cols] = low(d_p, v).astype(BF16)
+            own = slice(h * rows, (h + 1) * rows)
+            mixed = dot(jnp.concatenate([p[own], d_p[own]], axis=0), values[:reach, cols]).astype(BF16)
+            attended[0, span, cols] = mixed[:rows]
+            attended[1, span, cols] = mixed[rows:]
 
     def project(c):
         first, rows = chunks[c]
@@ -335,6 +386,10 @@
         out_send[span, :] = dot(attended[other, span, :], wo[...]).astype(BF16)
         pair_copy(c).start()
         own_part[span, :] = dot(attended[kind, span, :], wo[...])
+
+    def forward(c):
+        first, rows = chunks[c]
+        span = slice(first, first + rows)
         pair_copy(c).wait_recv()
         summed = own_part[span, :] + pair_recv[span, :].astype(F32)
         own_part[span, :] = summed
@@ -381,7 +436,7 @@
     def arrive(c, h):
         for slot in range(lines):
             gap = outer - slot
-            far = gap if isinstance(gap, int) else jnp.abs(gap)
+            far = jnp.abs(gap)
             onward = jnp.where(gap > 0, outer + 1 < lines, outer >= 1)
             passed = (lax.rem(far, 2) == 0) & onward
 
@@ -408,21 +463,34 @@
         back_tangent = jnp.where(kind == 0, back_other, back_own).astype(BF16)
         cos_q = cos[span, :]
         sin_q = sin[span, :]
+        u, u_tangent = [], []
+        for h in range(heads):
+            cols = slice(h * HEAD_DIM, (h + 1) * HEAD_DIM)
+            pulled = dot(
+                jnp.concatenate([back[:, cols], back_tangent[:, cols]], axis=0), values[:reach, cols], NT
+            )
+            u.append(pulled[:rows])
+            u_tangent.append(pulled[rows:])
+        u = jnp.concatenate(u, axis=0)
+        u_tangent = jnp.concatenate(u_tangent, axis=0)
+        p = soft[:, span, :reach].reshape(heads * rows, reach)
+        d_p = d_soft[:, span, :reach].reshape(heads * rows, reach)
+        centered = u - jnp.sum(p * u, axis=1, keepdims=True)
+        level = jnp.sum(d_p * u + p * u_tangent, axis=1, keepdims=True)
+        all_mixed = ((d_p * centered + p * (u_tangent - level)) * scale).astype(BF16)
+        all_lead = (p * centered * scale).astype(BF16)
         for h in range(heads):
             cols = slice(h * HEAD_DIM, (h + 1) * HEAD_DIM)
             left = left_main[h, span, :]
             right = right_main[h, :reach, :]
-            v = values[:reach, cols]
-            p = soft[h, span, :reach]
-            d_p = d_soft[h, span, :reach]
-            u = dot(back[:, cols], v, NT)
-            u_tangent = dot(back_tangent[:, cols], v, NT)
-            centered = u - jnp.sum(p * u, axis=1, keepdims=True)
-            level = jnp.sum(d_p * u + p * u_tangent, axis=1, keepdims=True)
-            mixed = ((d_p * centered + p * (u_tangent - level)) * scale).astype(BF16)
-            lead = (p * centered * scale).astype(BF16)
+            mixed = all_mixed[h * rows : (h + 1) * rows]
+            lead = all_lead[h * rows : (h + 1) * rows]
             hq = dot(mixed, right[:, :HEAD_DIM]) + dot(lead, right[:, HEAD_DIM:])
-            hk = dot(mixed, left[:, HEAD_DIM:], TN) + dot(lead, left[:, :HEAD_DIM], TN)
+            hk = dot(
+                jnp.concatenate([mixed, lead], axis=0),
+                jnp.concatenate([left[:, HEAD_DIM:], left[:, :HEAD_DIM]], axis=0),
+                TN,
+            )
             if c > 0:
                 hk = hk_sum[:reach, cols] + hk
             if c < count - 1:
@@ -438,25 +506,39 @@
             sums[0] = sums[0] + jnp.sum(hq.astype(F32) * probe, axis=0, keepdims=True)
             sums[1] = sums[1] + jnp.sum(hk.astype(F32) * probe, axis=0, keepdims=True)
 
+    def gather_slabs():
+        for step in range(1, lines):
+            slab_copy(step).wait_recv()
+            share_copy(step).start()
+        slabs[outer] = signed[:, pl.ds(pl.multiple_of(outer * slab, slab), slab)]
+
+    def turn_slabs():
+        for step in range(1, lines):
+            share_copy(step).wait_recv()
+        for o in range(lines):
+            slabs_turned[:, o * seq : (o + 1) * seq] = jnp.transpose(slabs[o])
+
     attend(0)
     loads[4].wait()
     project(0)
-    for c in range(1, count):
+    forward(0)
+    for c in (1, 2):
         attend(c)
         project(c)
+        forward(c)
     loads[5].wait()
     wo_turned[...] = jnp.transpose(wo[...])
-    for step in range(1, lines):
-        slab_copy(step).wait_recv()
-        share_copy(step).start()
-    slabs[outer] = signed[:, pl.ds(pl.multiple_of(outer * slab, slab), slab)]
-
     curve(0)
-    for step in range(1, lines):
-        share_copy(step).wait_recv()
-    for o in range(lines):
-        slabs_turned[:, o * seq : (o + 1) * seq] = jnp.transpose(slabs[o])
-    for c in range(1, count):
+    for c in range(3, count):
+        attend(c)
+        project(c)
+        forward(c)
+    gather_slabs()
+    curve(1)
+    for h in range(heads):
+        relay(0, h)
+    turn_slabs()
+    for c in range(2, count):
         curve(c)
         for h in range(heads):
             relay(c - 1, h)
@@ -504,6 +586,12 @@
     peer_rows = pl.ds(pl.multiple_of((1 - inner) * block, block), block)
     for h in range(heads):
         relay(count - 1, h)
+        for c in range(count):
+            arrive(c, h)
+        stack = gathered[h].reshape(lines * seq, PAIR)
+        x_send[h] = dot(slabs_turned[peer_rows, :], stack).astype(BF16)
+        x_copy(h).start()
+        own_sum[h] = dot(slabs_turned[own_rows, :], stack)
         if h < 3:
             stat_copy(h).wait_recv()
             total = stat_send[h] + stat_recv[h]
@@ -514,13 +602,6 @@
                 stat_all[outer] = total
                 for step in range(1, lines):
                     all_copy(step).start()
-    for h in range(heads):
-        for c in range(count):
-            arrive(c, h)
-        stack = gathered[h].reshape(lines * seq, PAIR)
-        x_send[h] = dot(slabs_turned[peer_rows, :], stack).astype(BF16)
-        x_copy(h).start()
-        own_sum[h] = dot(slabs_turned[own_rows, :], stack)
 
     def out_copies(h):
         cols = pl.ds(h * HEAD_DIM, HEAD_DIM)
@@ -561,6 +642,26 @@
         x_copy(h).wait_send()
         for copy in out_copies(h):
             copy.wait()
+
+
+def finish(query_in, key_in, mean_in, query_out, key_out, mean_out, held, sem):
+    rows = query_in.shape[0] // 2
+    moves = []
+    for n, (source, target) in enumerate(((query_in, query_out), (key_in, key_out))):
+        for part in range(2):
+            span = pl.ds(part * rows, rows)
+            slot = held.at[n, span, :]
+            take = pltpu.make_async_copy(source.at[span, :], slot, sem.at[0, n, part])
+            give = pltpu.make_async_copy(slot, target.at[span, :], sem.at[1, n, part])
+            take.start()
+            moves.append((take, give))
+    mean_out[0] = mean_in[0, 0]
+    mean_out[1] = mean_in[0, HEAD_DIM // 2]
+    for take, give in moves:
+        take.wait()
+        give.start()
+    for take, give in moves:
+        give.wait()
 
 
 def local(
@@ -584,8 +685,8 @@
     heads = feat // HEAD_DIM
     block = width // groups
     lines = groups // 2
-    quarter = seq // 4
-    chunks = ((3 * quarter, quarter), (2 * quarter, quarter), (0, 2 * quarter))
+    sizes = [part * seq // 16 for part in SIZES]
+    chunks = tuple((seq - sum(sizes[: n + 1]), size) for n, size in enumerate(sizes))
     count = len(chunks)
     position = np.arange(seq, dtype=np.float32)
     exponent = np.arange(0, HEAD_DIM, 2).astype(np.float32) / np.float32(HEAD_DIM)
@@ -605,9 +706,16 @@
             jax.ShapeDtypeStruct((block, feat), F32),
             jax.ShapeDtypeStruct((1, HEAD_DIM), F32),
         ),
-        in_specs=[vmem] * 7 + [anywhere] * 6,
+        in_specs=[pl.BlockSpec(memory_space=pltpu.HBM)] * 13,
         out_specs=(anywhere, anywhere, vmem),
         scratch_shapes=[
+            pltpu.VMEM((1, seq), F32),
+            pltpu.VMEM((1, seq), jnp.int32),
+            pltpu.VMEM((1, width), jnp.int32),
+            pltpu.VMEM((1, 2, feat), jnp.int32),
+            pltpu.VMEM((1, width), F32),
+            pltpu.VMEM((seq, HEAD_DIM), F32),
+            pltpu.VMEM((seq, HEAD_DIM), F32),
             pltpu.VMEM((seq, width), BF16),
             pltpu.VMEM((seq, width), BF16),
             pltpu.VMEM((width, feat), BF16),
@@ -664,9 +772,10 @@
             dma((lines,)),
             dma((lines,)),
             dma((2, heads)),
+            dma((7,)),
         ],
         compiler_params=pltpu.CompilerParams(
-            collective_id=0, has_side_effects=True, vmem_limit_bytes=58 * 1024 * 1024
+            collective_id=0, has_side_effects=True, vmem_limit_bytes=62 * 1024 * 1024
         ),
     )(
         loss_weights.reshape(1, seq),
@@ -683,8 +792,17 @@
         w_value,
         w_out,
     )
-    mean_diag = jnp.stack([means[0, 0], means[0, HEAD_DIM // 2]])
-    return (diag_query, diag_key, mean_diag)
+    return pl.pallas_call(
+        finish,
+        out_shape=(
+            jax.ShapeDtypeStruct((block, feat), F32),
+            jax.ShapeDtypeStruct((block, feat), F32),
+            jax.ShapeDtypeStruct((2,), F32),
+        ),
+        in_specs=[anywhere, anywhere, pl.BlockSpec(memory_space=pltpu.SMEM)],
+        out_specs=(anywhere, anywhere, pl.BlockSpec(memory_space=pltpu.SMEM)),
+        scratch_shapes=[pltpu.VMEM((2, block, feat), F32), dma((2, 2, 2))],
+    )(diag_query, diag_key, means)
 
 
 def solution(mesh):

time: 84.3 us -> 76.6 us (0.909)
  local copies, waits for them, and re-layouts: 5.02 us -> 0 us
  other arithmetic: 1.88 us -> 0 us
  Pallas kernels: 76.5 us -> 75.6 us
    pallas_call x1, Pallas kernels: 76.5 us -> 72.5 us  [local(): pl.pallas_call(functools.partial(kernel, groups, parts, float(width * fea...]
    unnamed x2 -> x0, local copies, waits for them, and re-layouts: 3.73 us -> none
    pallas_call x0 -> x1, Pallas kernels: none -> 3.16 us  [local(): pl.pallas_call(finish, out_shape=(jax.ShapeDtypeStruct((block, feat), F32...]
    another operation x1 -> x0, other arithmetic: 1.88 us -> none  [local(): mean_diag = jnp.stack([means[0, 0], means[0, HEAD_DIM // 2]])]
    slice x1 -> x0, local copies, waits for them, and re-layouts: 1.28 us -> none  [local(): mean_diag = jnp.stack([means[0, 0], means[0, HEAD_DIM // 2]])]
where the time goes in v2:
time: 76.6 us; the launch traced here: 76.4 us
  Pallas kernels  75.6 us (99%)
  between operations  0.8 us (1%)
    pallas_call x1, Pallas kernels, local(): pl.pallas_call(functools.partial(kernel, groups, parts, float(width * fea...  72.5 us
    pallas_call x1, Pallas kernels, local(): pl.pallas_call(finish, out_shape=(jax.ShapeDtypeStruct((block, feat), F32...  3.16 us

profile of v2, /device:TPU:0, one launch (start us, length us, event | category | flops | bytes accessed | tf_op | source)
XLA Modules:
  0.0 76.4 jit_solution(3774678237727713551)
XLA Ops:
  0.6 72.5 %shard_map.148 = (f32[256,512]{1,0:T(8,128)}, f32[256,512]{1,0:T(8,128)}, f32[1,128]{1,0:T(1,128)}) custom-call(f32[1,256]{1,0:T(1,128)} %bitcast.3, s32[1,256]{1,0:T(1,128)} %seg_hbm.1, s32[1,2048]{1,0:T(1,128)} %model_hbm.1, s32[1,2,512]{2,1,0:T(2,128)} %head_hbm.1, f32[1,2048]{1,0:T(1,128)} %bitcast.2, f32[256,128]{1,0:T(8,128)} %constant.4.clone.cosine_hbm, ...), custom_call_target="tpu_custom_call" | custom-call | tf_op jit(solution)/shard_map/pallas_call | solution.py:702
  73.1 3.2 %shard_map.149 = (f32[256,512]{1,0:T(8,128)}, f32[256,512]{1,0:T(8,128)}, f32[2]{0:T(128)}) custom-call(f32[256,512]{1,0:T(8,128)} %get-tuple-element.6.query_in, f32[256,512]{1,0:T(8,128)} %get-tuple-element.7.key_in, f32[1,128]{1,0:T(1,128)} %get-tuple-element.8.mean_in), custom_call_target="tpu_custom_call" | custom-call | tf_op jit(solution)/shard_map/pallas_call | solution.py:795

commit v3 on v2

--- a/solution.py
+++ b/solution.py
@@ -411,8 +411,11 @@
     def line_wait(c, h, slot):
         line_copy(c, h, slot, outer, 0).wait_recv()
 
-    def own_sends(c, h, act):
+    def own_sends(c, h, act, near=True, far=True):
         for way, hop in enumerate((2, -2, 1, -1)):
+            if not (near if abs(hop) == 1 else far):
+                continue
+
             @pl.when((outer + hop >= 0) & (outer + hop < lines))
             def _():
                 act(line_copy(c, h, outer, outer + hop, way))
@@ -501,7 +504,7 @@
             hk = (hk.astype(BF16).astype(F32) * head_sign[1:2, cols]).astype(BF16)
             gathered[h, outer, span, :HEAD_DIM] = hq
             gathered[h, outer, span, HEAD_DIM:] = hk
-            own_sends(c, h, lambda copy: copy.start())
+            own_sends(c, h, lambda copy: copy.start(), near=c < count - 1)
             probe = product[span, cols]
             sums[0] = sums[0] + jnp.sum(hq.astype(F32) * probe, axis=0, keepdims=True)
             sums[1] = sums[1] + jnp.sum(hk.astype(F32) * probe, axis=0, keepdims=True)
@@ -585,7 +588,9 @@
     own_rows = pl.ds(pl.multiple_of(inner * block, block), block)
     peer_rows = pl.ds(pl.multiple_of((1 - inner) * block, block), block)
     for h in range(heads):
+        own_sends(count - 1, h, lambda copy: copy.start(), far=False)
         relay(count - 1, h)
+    for h in range(heads):
         for c in range(count):
             arrive(c, h)
         stack = gathered[h].reshape(lines * seq, PAIR)

time: 76.6 us -> 74.6 us (0.974)
  Pallas kernels: 75.6 us -> 73.6 us
    pallas_call x1, Pallas kernels: 72.5 us -> 70.5 us  [local(): pl.pallas_call(functools.partial(kernel, groups, parts, float(width * fea...]
where the time goes in v3:
time: 74.6 us; the launch traced here: 74.4 us
  Pallas kernels  73.6 us (99%)
  between operations  0.8 us (1%)
    pallas_call x1, Pallas kernels, local(): pl.pallas_call(functools.partial(kernel, groups, parts, float(width * fea...  70.5 us
    pallas_call x1, Pallas kernels, local(): pl.pallas_call(finish, out_shape=(jax.ShapeDtypeStruct((block, feat), F32...  3.16 us

profile of v3, /device:TPU:0, one launch (start us, length us, event | category | flops | bytes accessed | tf_op | source)
XLA Modules:
  0.0 74.4 jit_solution(1005709550993339549)
XLA Ops:
  0.6 70.5 %shard_map.148 = (f32[256,512]{1,0:T(8,128)}, f32[256,512]{1,0:T(8,128)}, f32[1,128]{1,0:T(1,128)}) custom-call(f32[1,256]{1,0:T(1,128)} %bitcast.3, s32[1,256]{1,0:T(1,128)} %seg_hbm.1, s32[1,2048]{1,0:T(1,128)} %model_hbm.1, s32[1,2,512]{2,1,0:T(2,128)} %head_hbm.1, f32[1,2048]{1,0:T(1,128)} %bitcast.2, f32[256,128]{1,0:T(8,128)} %constant.4.clone.cosine_hbm, ...), custom_call_target="tpu_custom_call" | custom-call | tf_op jit(solution)/shard_map/pallas_call | solution.py:707
  71.1 3.2 %shard_map.149 = (f32[256,512]{1,0:T(8,128)}, f32[256,512]{1,0:T(8,128)}, f32[2]{0:T(128)}) custom-call(f32[256,512]{1,0:T(8,128)} %get-tuple-element.6.query_in, f32[256,512]{1,0:T(8,128)} %get-tuple-element.7.key_in, f32[1,128]{1,0:T(1,128)} %get-tuple-element.8.mean_in), custom_call_target="tpu_custom_call" | custom-call | tf_op jit(solution)/shard_map/pallas_call | solution.py:800

commit v4 on v3

--- a/solution.py
+++ b/solution.py
@@ -590,13 +590,6 @@
     for h in range(heads):
         own_sends(count - 1, h, lambda copy: copy.start(), far=False)
         relay(count - 1, h)
-    for h in range(heads):
-        for c in range(count):
-            arrive(c, h)
-        stack = gathered[h].reshape(lines * seq, PAIR)
-        x_send[h] = dot(slabs_turned[peer_rows, :], stack).astype(BF16)
-        x_copy(h).start()
-        own_sum[h] = dot(slabs_turned[own_rows, :], stack)
         if h < 3:
             stat_copy(h).wait_recv()
             total = stat_send[h] + stat_recv[h]
@@ -607,6 +600,13 @@
                 stat_all[outer] = total
                 for step in range(1, lines):
                     all_copy(step).start()
+    for h in range(heads):
+        for c in range(count):
+            arrive(c, h)
+        stack = gathered[h].reshape(lines * seq, PAIR)
+        x_send[h] = dot(slabs_turned[peer_rows, :], stack).astype(BF16)
+        x_copy(h).start()
+        own_sum[h] = dot(slabs_turned[own_rows, :], stack)
 
     def out_copies(h):
         cols = pl.ds(h * HEAD_DIM, HEAD_DIM)

time: 74.6 us -> 74.6 us (level)
  no operation moved by 1% of the time
where the time goes in v4:
time: 74.6 us; the launch traced here: 74.4 us
  Pallas kernels  73.6 us (99%)
  between operations  0.8 us (1%)
    pallas_call x1, Pallas kernels, local(): pl.pallas_call(functools.partial(kernel, groups, parts, float(width * fea...  70.5 us
    pallas_call x1, Pallas kernels, local(): pl.pallas_call(finish, out_shape=(jax.ShapeDtypeStruct((block, feat), F32...  3.16 us

profile of v4, /device:TPU:0, one launch (start us, length us, event | category | flops | bytes accessed | tf_op | source)
XLA Modules:
  0.0 74.4 jit_solution(4559762251440735149)
XLA Ops:
  0.6 70.5 %shard_map.148 = (f32[256,512]{1,0:T(8,128)}, f32[256,512]{1,0:T(8,128)}, f32[1,128]{1,0:T(1,128)}) custom-call(f32[1,256]{1,0:T(1,128)} %bitcast.3, s32[1,256]{1,0:T(1,128)} %seg_hbm.1, s32[1,2048]{1,0:T(1,128)} %model_hbm.1, s32[1,2,512]{2,1,0:T(2,128)} %head_hbm.1, f32[1,2048]{1,0:T(1,128)} %bitcast.2, f32[256,128]{1,0:T(8,128)} %constant.4.clone.cosine_hbm, ...), custom_call_target="tpu_custom_call" | custom-call | tf_op jit(solution)/shard_map/pallas_call | solution.py:707
  71.1 3.2 %shard_map.149 = (f32[256,512]{1,0:T(8,128)}, f32[256,512]{1,0:T(8,128)}, f32[2]{0:T(128)}) custom-call(f32[256,512]{1,0:T(8,128)} %get-tuple-element.6.query_in, f32[256,512]{1,0:T(8,128)} %get-tuple-element.7.key_in, f32[1,128]{1,0:T(1,128)} %get-tuple-element.8.mean_in), custom_call_target="tpu_custom_call" | custom-call | tf_op jit(solution)/shard_map/pallas_call | solution.py:800
